TPU v7x, 128 devices: a whole 4x4x4 slice. The times are simulated.
128 devices in a mesh: row: 4 (over x_hi, core), col: 32 (over z, y, x_lo).
Axes of the slice: x: 4 (x_hi: 2, x_lo: 2; x = x_hi * 2 + x_lo), y: 4, z: 4, core: 2. Of those that a mesh axis runs over, the one named last changes fastest.
Arguments:
- rows: bfloat16 [4096, 4096], P(('row', 'col')), may hold values from -6 to 6
- task_ids: int32 [4096], P(('row', 'col')), may hold values from 0 to 8, as said below
- task_embed: bfloat16 [8, 4096], replicated, may hold values from -6 to 6
- norm_gain: float32 [4, 4096], replicated, may hold values from 0.1 to 1.9
- layer_weight: bfloat16 [4, 4096, 4096], P(None, None, 'col'), may hold values from -0.09375 to 0.09375
Outputs:
- packed_out: bfloat16 [4096, 4096], P('row', 'col')
Inputs may be any that keep to these rules, and one draw needn't show every extreme that they name: `task_ids`: 8 marks an empty row, smaller values name a task.
All inputs are finite; a program needn't handle non-finite values.
Results may differ from a plain program's by a relative error of at most 0.008.
Values may be sent and summed in bfloat16 or wider, within the bound.
A program may use at most 128 MiB of HBM per device.

v0:
```python
import jax
import jax.numpy as jnp
from jax import lax
from jax.sharding import Mesh
from jax.sharding import PartitionSpec as P

COL = ("col_0", "col_1", "col_2")
ROW_COL = ("row", "col_0", "col_1", "col_2")
epsilon = 1e-06


def from_everyone(x, axis):
    size = lax.axis_size(axis)
    return lax.all_to_all(jnp.broadcast_to(x[None], (size, *x.shape)), axis, 0, 0, tiled=True)


def folded_in_pairs(pieces, combine):
    while len(jax.tree.leaves(pieces)[0]) > 1:
        pieces = jax.vmap(combine)(*(pieces[side::2] for side in (0, 1)))
    return pieces[0]


def entering(x, axis, combine, identity):
    size, index = (lax.axis_size(axis), lax.axis_index(axis))
    passed = jnp.arange(size) < index

    def kept(part, zero, own):
        part = jnp.where(
            passed.reshape(-1, *(1 for _ in own.shape)), part, jnp.asarray(zero, own.dtype)
        )
        return part

    pieces = from_everyone(x, axis)
    return folded_in_pairs(kept(pieces, identity, x), combine)


def taken_together(x, axis):
    return from_everyone(x, axis).sum(axis=0)


def rows_for(lines, size):
    spare = -len(lines) % size
    return jnp.pad(lines, [(0, spare)] + [(0, 0)] * (lines.ndim - 1))


def own_block(blocks, axes, turns):
    dims = [lax.axis_size(a) for a in axes]
    blocks = blocks.reshape(*dims, *blocks.shape[1:])
    blocks = blocks.transpose(*turns, *range(len(axes), blocks.ndim))
    blocks = blocks.reshape(-1, *blocks.shape[len(axes) :])
    for k in turns:
        blocks = lax.psum_scatter(blocks, axes[k], scatter_dimension=0, tiled=True)
    return blocks[0]


def all_blocks(x, axes, turns):
    blocks = x
    for k in turns:
        blocks = lax.all_gather(blocks, axes[k])
    done = turns[::-1]
    back = [done.index(k) for k in range(len(axes))]
    blocks = blocks.transpose(*back, *range(len(axes), blocks.ndim))
    return blocks.reshape(-1, *x.shape)


def total_of(x, axes, turns):
    size, lines = (lax.axis_size(axes), x.reshape(-1, *x.shape[1:][-1:]))
    blocks = rows_for(lines, size).reshape(size, -1, *lines.shape[1:])
    own = own_block(blocks, axes, turns)
    whole = all_blocks(own, axes, turns[::-1]).reshape(-1, *lines.shape[1:])
    return whole[: len(lines)].reshape(x.shape)


def add_counts(earlier, later):
    return earlier + later


def activate_rows(hidden, gain):
    total_rows = hidden.shape[0]
    width = hidden.shape[1]
    block_rows = min(512, total_rows)

    def one_block(block):
        values = block.astype(jnp.float32)
        inverse_rms = lax.rsqrt(jnp.mean(values * values, axis=1, keepdims=True) + epsilon)
        return jax.nn.silu(values * inverse_rms * gain[None, :]).astype(jnp.bfloat16)

    blocks = hidden.reshape(total_rows // block_rows, block_rows, width)
    return lax.map(one_block, blocks).reshape(total_rows, width)


def shards(rows, task_ids, task_embed, norm_gain, layer_weight):
    row_count = rows.shape[0]
    width = rows.shape[1]
    task_count = task_embed.shape[0]
    row_devices = lax.axis_size("row")
    col_devices = lax.axis_size(COL)
    capacity = row_count // row_devices + task_count
    slots_group = row_count * col_devices
    task_range = jnp.arange(task_count, dtype=jnp.int32)
    member = (task_ids[:, None] == task_range[None, :]).astype(jnp.int32)
    counts = jnp.sum(member, axis=0)
    zero_counts = jnp.zeros_like(counts)
    before_col = entering(counts, COL, add_counts, zero_counts)
    row_total = taken_together(counts, COL)
    before_row = entering(row_total, "row", add_counts, zero_counts)
    totals = taken_together(row_total, "row")
    before = before_row + before_col
    task_base = jnp.cumsum(totals) - totals
    positions = jnp.arange(row_count, dtype=jnp.int32)
    earlier_mask = positions[None, :] < positions[:, None]
    same_task = task_ids[:, None] == task_ids[None, :]
    task_rank = jnp.sum((same_task & earlier_mask).astype(jnp.int32), axis=1)
    row_live = task_ids < task_count
    packed_pos = (
        jnp.sum(member * (task_base + before)[None, :], axis=1).astype(jnp.int32) + task_rank
    )
    target_row = packed_pos % row_devices
    slot_index = packed_pos // row_devices
    before_pos = packed_pos[None, :] < packed_pos[:, None]
    same_target = (target_row[:, None] == target_row[None, :]) & row_live[None, :]
    within = jnp.sum((same_target & before_pos).astype(jnp.int32), axis=1)
    send_at = jnp.where(row_live, target_row * capacity + within, -1)
    buffer_range = jnp.arange(row_devices * capacity, dtype=jnp.int32)
    select = buffer_range[:, None] == send_at[None, :]
    send_rows = jnp.dot(
        select.astype(jnp.bfloat16), rows, preferred_element_type=jnp.float32
    ).astype(jnp.bfloat16)
    send_rows = send_rows.reshape(row_devices, capacity, width)
    send_slots = jnp.sum(jnp.where(select, slot_index[None, :] + 1, 0), axis=1) - 1
    send_slots = send_slots.reshape(row_devices, capacity)
    got_rows, got_slots = (
        lax.all_to_all(send_rows, "row", split_axis=0, concat_axis=0, tiled=True),
        lax.all_to_all(send_slots, "row", split_axis=0, concat_axis=0, tiled=True),
    )
    got_rows = got_rows.reshape(row_devices * capacity, width)
    got_slots = got_slots.reshape(row_devices * capacity)
    slot_range = jnp.arange(slots_group, dtype=jnp.int32)
    placing = (slot_range[:, None] == got_slots[None, :]).astype(jnp.bfloat16)
    local_part = jnp.dot(placing, got_rows, preferred_element_type=jnp.float32).astype(jnp.bfloat16)
    placed = total_of(local_part, COL, (0, 1, 2)).astype(jnp.float32)
    group_index = lax.axis_index("row")
    slot_pos = slot_range * row_devices + group_index
    in_task = (slot_pos[:, None] >= task_base[None, :]) & (
        slot_pos[:, None] < (task_base + totals)[None, :]
    )
    task_term = jnp.dot(
        in_task.astype(jnp.bfloat16), task_embed, preferred_element_type=jnp.float32
    )
    hidden = (placed + task_term).astype(jnp.bfloat16)
    part_width = width // col_devices
    column = lax.axis_index(COL) * part_width
    layers = layer_weight.shape[0]
    result = hidden
    for layer_index in range(layers):
        active = activate_rows(hidden, norm_gain[layer_index])
        update = jnp.dot(active, layer_weight[layer_index], preferred_element_type=jnp.float32)
        own_cols = lax.dynamic_slice_in_dim(hidden, column, part_width, 1).astype(jnp.float32)
        result = (own_cols + update).astype(jnp.bfloat16)
        if layer_index + 1 < layers:
            hidden = lax.all_gather(result, COL, axis=1, tiled=True)
    return result


def solution(mesh):
    finer = Mesh(
        mesh.devices.reshape(mesh.shape["row"], 4, 4, 2), ("row", "col_0", "col_1", "col_2")
    )
    return jax.shard_map(
        shards,
        mesh=finer,
        in_specs=(P(ROW_COL, None), P(ROW_COL), P(), P(), P(None, None, COL)),
        out_specs=P("row", COL),
        check_vma=False,
    )
```

profile of v0, /device:TPU:0, one launch (start us, length us, event | category | flops | bytes accessed | tf_op | source)
XLA Modules:
  0.0 1077.1 jit_solution(16607815354569057039)
XLA Ops:
  7.9 9.4 all-to-all-start
  18.9 6.6 all-to-all-done
  26.4 4.0 all-to-all-start.1
  30.4 5.2 all-to-all-done.1
  38.4 3.2 all-to-all-start.2
  41.7 1.2 convolution_convert_fusion.1
  42.9 4.0 all-to-all-done.2
  46.9 3.5 all-to-all-start.3
  51.6 9.0 all-to-all-done.3
  60.6 5.5 convolution_convert_fusion
  66.2 76.0 %reduce-scatter.4.cloned.1.call-done = bf16[8,32,4096]{2,1,0:T(8,128)(2,1)} async-done(((bf16[32,32,4096]{2,1,0:T(8,128)(2,1)}), bf16[8,32,4096]{2,1,0:T(8,128)(2,1)}) %reduce-scatter.4.cloned.1.call-update) | async-done | bytes 2097168 | tf_op jit(solution)/shard_map/reduce_scatter | solution.py:52
  142.3 31.7 %reduce-scatter.6.cloned.1.call-done = bf16[2,32,4096]{2,1,0:T(8,128)(2,1)} async-done(((bf16[8,32,4096]{2,1,0:T(8,128)(2,1)}), bf16[2,32,4096]{2,1,0:T(8,128)(2,1)}) %reduce-scatter.6.cloned.1.call-update) | async-done | bytes 524304 | tf_op jit(solution)/shard_map/reduce_scatter | solution.py:52
  174.1 19.2 %reduce-scatter.8.cloned.1.call-done = bf16[1,32,4096]{2,1,0:T(8,128)(2,1)} async-done(((bf16[2,32,4096]{2,1,0:T(8,128)(2,1)}), bf16[1,32,4096]{2,1,0:T(8,128)(2,1)}) %reduce-scatter.8.cloned.1.call-update) | async-done | bytes 262160 | tf_op jit(solution)/shard_map/reduce_scatter | solution.py:52
  193.2 10.2 all_gather.24
  203.6 32.5 %all-gather.14.cloned.1.call-done = bf16[8,32,4096]{2,1,0:T(8,128)(2,1)} async-done(((bf16[2,32,4096]{2,1,0:T(8,128)(2,1)}), bf16[8,32,4096]{2,1,0:T(8,128)(2,1)}) %all-gather.14.cloned.1.call-update) | async-done | bytes 2097168 | tf_op jit(solution)/shard_map/all_gather | solution.py:59
  236.4 84.5 %all-gather.16.cloned.1.call-done = bf16[16,2,32,4096]{3,2,1,0:T(8,128)(2,1)} async-done(((bf16[4,2,32,4096]{3,2,1,0:T(8,128)(2,1)}), bf16[16,2,32,4096]{3,2,1,0:T(8,128)(2,1)}) %all-gather.16.cloned.1.call-update) | async-done | bytes 8388624 | tf_op jit(solution)/shard_map/all_gather | solution.py:59
  320.9 9.1 fusion.36
  329.9 4.3 broadcast.240.clone.2
  334.2 17.3 %while.40 = (s32[]{:T(128)}, bf16[2,512,4096]{2,1,0:T(8,128)(2,1)}, bf16[2,512,4096]{2,1,0:T(8,128)(2,1)}, f32[1,4096]{1,0:T(1,128)S(1)}, s32[]{:T(128)}) while((s32[]{:T(128)}, bf16[2,512,4096]{2,1,0:T(8,128)(2,1)}, bf16[2,512,4096]{2,1,0:T(8,128)(2,1)}, f32[1,4096]{1,0:T(1,128)S(1)}, s32[]{:T(128)}) %tuple.89), condition=%wide.region_13.14_spmd, body=%wide.region_11.13_spmd.sunk | while | flops 23069184 | bytes 12608065 | solution.py:89
  334.2 3.1 fusion.77
  337.3 5.6 fusion.78
  342.8 3.1 fusion.77
  345.9 5.6 fusion.78
  351.5 6.8 fusion.37
  358.6 209.7 %all-gather.8.cloned.1.call-done = bf16[1024,4096]{1,0:T(8,128)(2,1)} async-done(((bf16[1024,128]{1,0:T(8,128)(2,1)}), bf16[1024,4096]{1,0:T(8,128)(2,1)}) %all-gather.8.cloned.1.call-update) | async-done | bytes 8388624 | tf_op jit(solution)/shard_map/all_gather | solution.py:161
  568.3 4.3 broadcast.240.clone.1
  572.6 17.3 %while.41 = (s32[]{:T(128)}, bf16[2,512,4096]{2,1,0:T(8,128)(2,1)}, bf16[2,512,4096]{2,1,0:T(8,128)(2,1)}, f32[1,4096]{1,0:T(1,128)S(1)}, s32[]{:T(128)}) while((s32[]{:T(128)}, bf16[2,512,4096]{2,1,0:T(8,128)(2,1)}, bf16[2,512,4096]{2,1,0:T(8,128)(2,1)}, f32[1,4096]{1,0:T(1,128)S(1)}, s32[]{:T(128)}) %tuple.91), condition=%wide.region_16.17_spmd, body=%wide.region_14.16_spmd.sunk | while | flops 23069184 | bytes 12608065 | solution.py:89
  572.6 3.1 fusion.79
  575.7 5.6 fusion.80
  581.2 3.1 fusion.79
  584.3 5.6 fusion.80
  589.9 6.8 fusion.38
  597.0 208.1 %all-gather.10.cloned.1.call-done = bf16[1024,4096]{1,0:T(8,128)(2,1)} async-done(((bf16[1024,128]{1,0:T(8,128)(2,1)}), bf16[1024,4096]{1,0:T(8,128)(2,1)}) %all-gather.10.cloned.1.call-update) | async-done | bytes 8388624 | tf_op jit(solution)/shard_map/all_gather | solution.py:161
  805.1 4.3 broadcast.240.clone
  809.4 17.3 %while.42 = (s32[]{:T(128)}, bf16[2,512,4096]{2,1,0:T(8,128)(2,1)}, bf16[2,512,4096]{2,1,0:T(8,128)(2,1)}, f32[1,4096]{1,0:T(1,128)S(1)}, s32[]{:T(128)}) while((s32[]{:T(128)}, bf16[2,512,4096]{2,1,0:T(8,128)(2,1)}, bf16[2,512,4096]{2,1,0:T(8,128)(2,1)}, f32[1,4096]{1,0:T(1,128)S(1)}, s32[]{:T(128)}) %tuple.92), condition=%wide.region_19.20_spmd, body=%wide.region_17.19_spmd.sunk | while | flops 23069184 | bytes 12608065 | solution.py:89
  809.4 3.1 fusion.81
  812.5 5.6 fusion.82
  818.0 3.1 fusion.81
  821.1 5.6 fusion.82
  826.7 6.8 fusion.39
  833.5 208.4 %all-gather.12.cloned.1.call-done = bf16[1024,4096]{1,0:T(8,128)(2,1)} async-done(((bf16[1024,128]{1,0:T(8,128)(2,1)}), bf16[1024,4096]{1,0:T(8,128)(2,1)}) %all-gather.12.cloned.1.call-update) | async-done | bytes 8388624 | tf_op jit(solution)/shard_map/all_gather | solution.py:161
  1041.9 4.3 broadcast.240
  1046.2 17.3 %while.43 = (s32[]{:T(128)}, bf16[2,512,4096]{2,1,0:T(8,128)(2,1)}, bf16[2,512,4096]{2,1,0:T(8,128)(2,1)}, f32[1,4096]{1,0:T(1,128)S(1)}, s32[]{:T(128)}) while((s32[]{:T(128)}, bf16[2,512,4096]{2,1,0:T(8,128)(2,1)}, bf16[2,512,4096]{2,1,0:T(8,128)(2,1)}, f32[1,4096]{1,0:T(1,128)S(1)}, s32[]{:T(128)}) %tuple.90), condition=%wide.region_22.23_spmd, body=%wide.region_20.22_spmd.sunk | while | flops 23069184 | bytes 12608065 | solution.py:89
  1046.2 3.1 fusion.83
  1049.3 5.6 fusion.84
  1054.8 3.1 fusion.83
  1057.9 5.6 fusion.84
  1063.5 6.8 fusion.40
  (74 shorter events, 9.2 us)
Async XLA Ops:
  6.5 35.1 %copy-start = (bf16[32,4096]{1,0:T(8,128)(2,1)S(1)}, bf16[32,4096]{1,0:T(8,128)(2,1)}, u32[]{:S(2)}) copy-start(bf16[32,4096]{1,0:T(8,128)(2,1)} %param.13) | copy-start | bytes 786436
  7.9 17.6 %all-to-all-start = ((s32[32,1,8]{2,1,0:T(1,128)}), s32[32,1,8]{2,1,0:T(1,128)S(1)}, u32[]{:S(2)}, u32[]{:S(2)}) async-start(s32[32,1,8]{2,1,0:T(1,128)} %broadcast_in_dim.43), calls=%async_computation | async-start | bytes 32768 | tf_op jit(solution)/shard_map/all_to_all | solution.py:14
  26.4 9.2 all-to-all-start.1
  38.4 8.4 all-to-all-start.2
  46.9 13.8 %all-to-all-start.3 = ((bf16[4,16,4096]{2,1,0:T(8,128)(2,1)}), bf16[4,16,4096]{2,1,0:T(8,128)(2,1)S(1)}, u32[]{:S(2)}, u32[]{:S(2)}) async-start(bf16[4,16,4096]{2,1,0:T(8,128)(2,1)} %bitcast.11), calls=%async_computation.3 | async-start | bytes 1048576 | tf_op jit(solution)/shard_map/all_to_all | solution.py:133
  50.3 91.9 %reduce-scatter.4.cloned.1.call-start = ((), (), s32[]{:S(2)}) async-start(), calls=%async_computation.7 | async-start | bytes 10485760 | tf_op jit(solution)/shard_map/reduce_scatter | solution.py:52
  66.2 170.2 %copy-start.3 = (f32[4,4096]{1,0:T(4,128)S(1)}, f32[4,4096]{1,0:T(4,128)}, u32[]{:S(2)}) copy-start(f32[4,4096]{1,0:T(4,128)} %param.16) | copy-start | bytes 196612
  66.2 254.7 %copy-start.2 = (bf16[8,4096]{1,0:T(8,128)(2,1)S(1)}, bf16[8,4096]{1,0:T(8,128)(2,1)}, u32[]{:S(2)}) copy-start(bf16[8,4096]{1,0:T(8,128)(2,1)} %param.15) | copy-start | bytes 196612
  66.2 107.8 %reduce-scatter.6.cloned.1.call-start = ((), (), s32[]{:S(2)}) async-start(), calls=%async_computation.8 | async-start | bytes 2621440 | tf_op jit(solution)/shard_map/reduce_scatter | solution.py:52
  142.3 51.0 %reduce-scatter.8.cloned.1.call-start = ((), (), s32[]{:S(2)}) async-start(), calls=%async_computation.9 | async-start | bytes 786432 | tf_op jit(solution)/shard_map/reduce_scatter | solution.py:52
  174.0 62.0 %all-gather.14.cloned.1.call-start = ((), (), s32[]{:S(2)}) async-start(), calls=%async_computation.13 | async-start | bytes 2621440 | tf_op jit(solution)/shard_map/all_gather | solution.py:59
  203.5 117.4 %all-gather.16.cloned.1.call-start = ((), (), s32[]{:S(2)}) async-start(), calls=%async_computation.14 | async-start | bytes 10485760 | tf_op jit(solution)/shard_map/all_gather | solution.py:59
  236.1 332.3 %all-gather.8.cloned.1.call-start = ((), (), s32[]{:S(2)}) async-start(), calls=%async_computation.10 | async-start | bytes 8650752 | tf_op jit(solution)/shard_map/all_gather | solution.py:161
  358.3 446.8 %all-gather.10.cloned.1.call-start = ((), (), s32[]{:S(2)}) async-start(), calls=%async_computation.11 | async-start | bytes 8650752 | tf_op jit(solution)/shard_map/all_gather | solution.py:161
  596.7 445.2 %all-gather.12.cloned.1.call-start = ((), (), s32[]{:S(2)}) async-start(), calls=%async_computation.12 | async-start | bytes 8650752 | tf_op jit(solution)/shard_map/all_gather | solution.py:161
  1063.5 6.8 copy-start.1
Sparse Core Ops, SparseCore 0:
  66.3 75.9 reduce-scatter.3
  144.7 29.2 reduce-scatter.5
  176.4 16.8 reduce-scatter.7
  203.6 32.3 all-gather.13
  237.6 83.2 all-gather.15
  358.4 209.8 all-gather.7
  596.8 208.2 all-gather.9
  833.6 208.2 all-gather.11
where the time goes:
time: 1080 us
  waiting for transfers between devices  895 us (83%)
  other arithmetic  74.6 us (7%)
  matrix products  42.9 us (4%)
  starting transfers between devices  21 us (2%)
  local copies, waits for them, and re-layouts  19.8 us (2%)
  between operations  13.6 us (1%)
    all_gather x3, waiting for transfers between devices, shards(): hidden = lax.all_gather(result, COL, axis=1, tiled=True)  626 us
    reduce_scatter x3, waiting for transfers between devices, own_block(): blocks = lax.psum_scatter(blocks, axes[k], scatter_dimension=0, tiled=True)  127 us
    all_gather x2, waiting for transfers between devices, all_blocks(): blocks = lax.all_gather(blocks, axes[k])  117 us
    dynamic_update_slice x8, other arithmetic, activate_rows(): return lax.map(one_block, blocks).reshape(total_rows, width)  44.6 us
    dot_general x4, matrix products, shards(): jnp.dot(active, layer_weight[layer_index], preferred_element_type=jnp.flo...  27.1 us
    reduce_sum x8, other arithmetic, one_block(): jnp.mean(values * values, axis=1, keepdims=True) + epsilon  24.6 us
  transfers between devices with their start and end apart: 12, of which 12 were waited for; matrix products, arithmetic and copies ran while one was open for 0% of the time, Pallas kernels for 0%

commit v1 on v0

--- a/solution.py
+++ b/solution.py
@@ -158,7 +158,9 @@
         own_cols = lax.dynamic_slice_in_dim(hidden, column, part_width, 1).astype(jnp.float32)
         result = (own_cols + update).astype(jnp.bfloat16)
         if layer_index + 1 < layers:
-            hidden = lax.all_gather(result, COL, axis=1, tiled=True)
+            hidden = jnp.concatenate(
+                lax.all_to_all(jnp.stack([result] * lax.axis_size(COL)), COL, 0, 0), axis=1
+            )
     return result
 
 

time: 1080 us -> 939 us (0.87)
  waiting for transfers between devices: 895 us -> 503 us
  blocking collectives: 10.2 us -> 124 us
  local copies, waits for them, and re-layouts: 19.8 us -> 131 us
  starting transfers between devices: 21 us -> 44.6 us
    all_gather x3 -> x0, waiting for transfers between devices: 626 us -> none  [shards(): hidden = lax.all_gather(result, COL, axis=1, tiled=True)]
    all_to_all x0 -> x2, waiting for transfers between devices: none -> 235 us  [shards(): lax.all_to_all(jnp.stack([result] * lax.axis_size(COL)), COL, 0, 0)]
    all_to_all x0 -> x1, blocking collectives: none -> 114 us  [shards(): lax.all_to_all(jnp.stack([result] * lax.axis_size(COL)), COL, 0, 0)]
    reshape x0 -> x6, local copies, waits for them, and re-layouts: none -> 59.5 us  [shards(): jnp.concatenate(lax.all_to_all(jnp.stack([result] * lax.axis_size(COL)),...]
    another operation x4 -> x10, local copies, waits for them, and re-layouts: 17 us -> 69 us  [the longest x3 39.9 us: activate_rows(): blocks = hidden.reshape(total_rows // block_rows, block_rows, width)]
    all_to_all x0 -> x2, starting transfers between devices: none -> 24.2 us  [shards(): lax.all_to_all(jnp.stack([result] * lax.axis_size(COL)), COL, 0, 0)]
  transfers between devices with their start and end apart: 12 -> 11, of which waited for: 12 -> 11; matrix products, arithmetic and copies ran while one was open for 0% -> 0% of each run, Pallas kernels for 0% -> 0%
where the time goes in v1:
time: 939 us; the launch traced here: 933 us
  waiting for transfers between devices  503 us (54%)
  local copies, waits for them, and re-layouts  131 us (14%)
  blocking collectives  124 us (13%)
  other arithmetic  74.6 us (8%)
  starting transfers between devices  44.6 us (5%)
  matrix products  40.8 us (4%)
  between operations  13.6 us (1%)
    all_to_all x2, waiting for transfers between devices, shards(): lax.all_to_all(jnp.stack([result] * lax.axis_size(COL)), COL, 0, 0)  235 us
    reduce_scatter x3, waiting for transfers between devices, own_block(): blocks = lax.psum_scatter(blocks, axes[k], scatter_dimension=0, tiled=True)  127 us
    all_gather x2, waiting for transfers between devices, all_blocks(): blocks = lax.all_gather(blocks, axes[k])  117 us
    all_to_all x1, blocking collectives, shards(): lax.all_to_all(jnp.stack([result] * lax.axis_size(COL)), COL, 0, 0)  114 us
    reshape x6, local copies, waits for them, and re-layouts, shards(): jnp.concatenate(lax.all_to_all(jnp.stack([result] * lax.axis_size(COL)),...  59.5 us
    dynamic_update_slice x8, other arithmetic, activate_rows(): return lax.map(one_block, blocks).reshape(total_rows, width)  44.6 us
    another operation x3, local copies, waits for them, and re-layouts, activate_rows(): blocks = hidden.reshape(total_rows // block_rows, block_rows, width)  39.9 us
    dot_general x4, matrix products, shards(): jnp.dot(active, layer_weight[layer_index], preferred_element_type=jnp.flo...  25 us
  transfers between devices with their start and end apart: 11, of which 11 were waited for; matrix products, arithmetic and copies ran while one was open for 0% of the time, Pallas kernels for 0%

profile of v1, /device:TPU:0, one launch (start us, length us, event | category | flops | bytes accessed | tf_op | source)
XLA Modules:
  0.0 933.2 jit_solution(4628540100985994374)
XLA Ops:
  7.9 9.4 %all-to-all-start = ((s32[32,1,8]{2,1,0:T(1,128)}), s32[32,1,8]{2,1,0:T(1,128)S(1)}, u32[]{:S(2)}, u32[]{:S(2)}) async-start(s32[32,1,8]{2,1,0:T(1,128)} %broadcast_in_dim.43), calls=%async_computation | async-start | bytes 32768 | tf_op jit(solution)/shard_map/all_to_all | solution.py:14
  18.9 6.6 all-to-all-done
  30.4 5.2 all-to-all-done.1
  51.6 9.0 all-to-all-done.3
  60.6 5.5 convolution_convert_fusion
  66.2 76.0 %reduce-scatter.4.cloned.1.call-done = bf16[8,32,4096]{2,1,0:T(8,128)(2,1)} async-done(((bf16[32,32,4096]{2,1,0:T(8,128)(2,1)}), bf16[8,32,4096]{2,1,0:T(8,128)(2,1)}) %reduce-scatter.4.cloned.1.call-update) | async-done | bytes 2097168 | tf_op jit(solution)/shard_map/reduce_scatter | solution.py:52
  142.3 31.7 %reduce-scatter.6.cloned.1.call-done = bf16[2,32,4096]{2,1,0:T(8,128)(2,1)} async-done(((bf16[8,32,4096]{2,1,0:T(8,128)(2,1)}), bf16[2,32,4096]{2,1,0:T(8,128)(2,1)}) %reduce-scatter.6.cloned.1.call-update) | async-done | bytes 524304 | tf_op jit(solution)/shard_map/reduce_scatter | solution.py:52
  174.1 19.2 %reduce-scatter.8.cloned.1.call-done = bf16[1,32,4096]{2,1,0:T(8,128)(2,1)} async-done(((bf16[2,32,4096]{2,1,0:T(8,128)(2,1)}), bf16[1,32,4096]{2,1,0:T(8,128)(2,1)}) %reduce-scatter.8.cloned.1.call-update) | async-done | bytes 262160 | tf_op jit(solution)/shard_map/reduce_scatter | solution.py:52
  193.2 10.2 %all_gather.15 = bf16[2,32,4096]{2,1,0:T(8,128)(2,1)} all-gather(bf16[1,32,4096]{2,1,0:T(8,128)(2,1)} %reduce-scatter.8.cloned.1.call-done), channel_id=1, replica_groups=mesh['row'=4,'col_0'=4,'col_1'=4,'col_2'=2] {'col_2'}, dimensions={0}, use_global_device_ids=true | all-gather | bytes 786432 | tf_op jit(solution)/shard_map/all_gather | solution.py:59
  203.7 32.3 %all-gather.5.cloned.1.call-done = bf16[8,32,4096]{2,1,0:T(8,128)(2,1)} async-done(((bf16[2,32,4096]{2,1,0:T(8,128)(2,1)}), bf16[8,32,4096]{2,1,0:T(8,128)(2,1)}) %all-gather.5.cloned.1.call-update) | async-done | bytes 2097168 | tf_op jit(solution)/shard_map/all_gather | solution.py:59
  236.2 84.7 %all-gather.7.cloned.1.call-done = bf16[16,2,32,4096]{3,2,1,0:T(8,128)(2,1)} async-done(((bf16[4,2,32,4096]{3,2,1,0:T(8,128)(2,1)}), bf16[16,2,32,4096]{3,2,1,0:T(8,128)(2,1)}) %all-gather.7.cloned.1.call-update) | async-done | bytes 8388624 | tf_op jit(solution)/shard_map/all_gather | solution.py:59
  320.9 9.1 fusion.36
  330.0 4.3 broadcast.246.clone.2
  334.2 17.3 %while.40 = (s32[]{:T(128)}, bf16[2,512,4096]{2,1,0:T(8,128)(2,1)}, bf16[2,512,4096]{2,1,0:T(8,128)(2,1)}, f32[1,4096]{1,0:T(1,128)S(1)}, s32[]{:T(128)}) while((s32[]{:T(128)}, bf16[2,512,4096]{2,1,0:T(8,128)(2,1)}, bf16[2,512,4096]{2,1,0:T(8,128)(2,1)}, f32[1,4096]{1,0:T(1,128)S(1)}, s32[]{:T(128)}) %tuple.83), condition=%wide.region_13.14_spmd, body=%wide.region_11.13_spmd.sunk | while | flops 23069184 | bytes 12608065 | solution.py:89
  337.3 5.6 fusion.81
  345.9 5.6 fusion.81
  351.5 6.1 fusion.37
  357.6 5.1 stack.6
  362.7 8.1 all-to-all-start.4
  370.8 122.6 %all-to-all-done.4 = bf16[32,1024,128]{2,1,0:T(8,128)(2,1)} async-done(((bf16[32,1024,128]{2,1,0:T(8,128)(2,1)}), bf16[32,1024,128]{2,1,0:T(8,128)(2,1)}, u32[]{:S(2)}, u32[]{:S(2)}) %all-to-all-start.4) | async-done | bytes 8388640 | tf_op jit(solution)/shard_map/all_to_all | solution.py:162
  493.4 12.0 %copy.25 = bf16[1024,32,128]{2,1,0:T(8,128)(2,1)} copy(bf16[1024,32,128]{2,0,1:T(8,128)(2,1)} %bitcast.20) | data formatting | bytes 16777216 | tf_op jit(solution)/shard_map/reshape | solution.py:161
  505.4 13.3 %reshape_reshape.10 = bf16[2,512,4096]{2,1,0:T(8,128)(2,1)} reshape(bf16[1024,32,128]{2,1,0:T(8,128)(2,1)} %copy.25) | data formatting | bytes 16777216 | tf_op jit(solution)/shard_map/reshape;reshape | solution.py:88
  518.7 4.3 broadcast.246.clone.1
  523.0 17.8 %while.41 = (s32[]{:T(128)}, bf16[2,512,4096]{2,1,0:T(8,128)(2,1)}, bf16[2,512,4096]{2,1,0:T(8,128)(2,1)}, f32[1,4096]{1,0:T(1,128)S(1)}, s32[]{:T(128)}) while((s32[]{:T(128)}, bf16[2,512,4096]{2,1,0:T(8,128)(2,1)}, bf16[2,512,4096]{2,1,0:T(8,128)(2,1)}, f32[1,4096]{1,0:T(1,128)S(1)}, s32[]{:T(128)}) %tuple.64), condition=%wide.region_16.17_spmd, body=%wide.region_14.16_spmd.sunk | while | flops 23069184 | bytes 12608065 | solution.py:89
  526.0 5.6 fusion.83
  534.7 5.6 fusion.83
  540.7 7.8 copy_bitcast_fusion.2
  548.6 6.1 fusion.38
  554.6 5.1 stack.7
  559.7 16.1 %all-to-all-start.5 = ((bf16[32,1024,128]{2,1,0:T(8,128)(2,1)}), bf16[32,1024,128]{2,1,0:T(8,128)(2,1)}, u32[]{:S(2)}, u32[]{:S(2)}) async-start(bf16[32,1024,128]{2,1,0:T(8,128)(2,1)} %stack.7), calls=%async_computation.8 | async-start | bytes 16777216 | tf_op jit(solution)/shard_map/all_to_all | solution.py:162
  575.9 112.0 %all-to-all-done.5 = bf16[32,1024,128]{2,1,0:T(8,128)(2,1)} async-done(((bf16[32,1024,128]{2,1,0:T(8,128)(2,1)}), bf16[32,1024,128]{2,1,0:T(8,128)(2,1)}, u32[]{:S(2)}, u32[]{:S(2)}) %all-to-all-start.5) | async-done | bytes 8388640 | tf_op jit(solution)/shard_map/all_to_all | solution.py:162
  687.9 12.0 %copy.27 = bf16[1024,32,128]{2,1,0:T(8,128)(2,1)} copy(bf16[1024,32,128]{2,0,1:T(8,128)(2,1)} %bitcast.23) | data formatting | bytes 16777216 | tf_op jit(solution)/shard_map/reshape | solution.py:161
  699.9 13.3 %reshape_reshape.11 = bf16[2,512,4096]{2,1,0:T(8,128)(2,1)} reshape(bf16[1024,32,128]{2,1,0:T(8,128)(2,1)} %copy.27) | data formatting | bytes 16777216 | tf_op jit(solution)/shard_map/reshape;reshape | solution.py:88
  713.2 4.3 broadcast.246.clone
  717.5 17.5 %while.42 = (s32[]{:T(128)}, bf16[2,512,4096]{2,1,0:T(8,128)(2,1)}, bf16[2,512,4096]{2,1,0:T(8,128)(2,1)}, f32[1,4096]{1,0:T(1,128)S(1)}, s32[]{:T(128)}) while((s32[]{:T(128)}, bf16[2,512,4096]{2,1,0:T(8,128)(2,1)}, bf16[2,512,4096]{2,1,0:T(8,128)(2,1)}, f32[1,4096]{1,0:T(1,128)S(1)}, s32[]{:T(128)}) %tuple.67), condition=%wide.region_19.20_spmd, body=%wide.region_17.19_spmd.sunk | while | flops 23069184 | bytes 12608065 | solution.py:89
  720.5 5.6 fusion.85
  729.2 5.6 fusion.85
  734.9 7.8 copy_bitcast_fusion.1
  742.8 6.1 fusion.39
  750.7 113.9 %all_to_all.46 = bf16[32,1024,128]{2,1,0:T(8,128)(2,1)} all-to-all(bf16[32,1024,128]{2,1,0:T(8,128)(2,1)S(1)} %stack.8), channel_id=1, replica_groups=mesh['row'=4,'col_0'=4,'col_1'=4,'col_2'=2] {'col_0','col_1','col_2'}, dimensions={0} | all-to-all | bytes 16777216 | tf_op jit(solution)/shard_map/all_to_all | solution.py:162
  864.7 12.0 %copy.29 = bf16[1024,32,128]{2,1,0:T(8,128)(2,1)} copy(bf16[1024,32,128]{2,0,1:T(8,128)(2,1)} %bitcast.78) | data formatting | bytes 16777216 | tf_op jit(solution)/shard_map/reshape | solution.py:161
  876.7 13.3 %reshape_reshape.12 = bf16[2,512,4096]{2,1,0:T(8,128)(2,1)} reshape(bf16[1024,32,128]{2,1,0:T(8,128)(2,1)} %copy.29) | data formatting | bytes 16777216 | tf_op jit(solution)/shard_map/reshape;reshape | solution.py:88
  890.0 4.3 broadcast.246
  894.2 17.5 %while.43 = (s32[]{:T(128)}, bf16[2,512,4096]{2,1,0:T(8,128)(2,1)}, bf16[2,512,4096]{2,1,0:T(8,128)(2,1)}, f32[1,4096]{1,0:T(1,128)S(1)}, s32[]{:T(128)}) while((s32[]{:T(128)}, bf16[2,512,4096]{2,1,0:T(8,128)(2,1)}, bf16[2,512,4096]{2,1,0:T(8,128)(2,1)}, f32[1,4096]{1,0:T(1,128)S(1)}, s32[]{:T(128)}) %tuple.70), condition=%wide.region_22.23_spmd, body=%wide.region_20.22_spmd.sunk | while | flops 23069184 | bytes 12608065 | solution.py:89
  897.3 5.6 fusion.87
  906.0 5.6 fusion.87
  911.8 7.9 copy_bitcast_fusion
  919.6 6.8 fusion.40
  (82 shorter events, 50.9 us)
Async XLA Ops:
  6.5 35.1 %copy-start = (bf16[32,4096]{1,0:T(8,128)(2,1)S(1)}, bf16[32,4096]{1,0:T(8,128)(2,1)}, u32[]{:S(2)}) copy-start(bf16[32,4096]{1,0:T(8,128)(2,1)} %param.13) | copy-start | bytes 786436
  7.9 17.6 %all-to-all-start = ((s32[32,1,8]{2,1,0:T(1,128)}), s32[32,1,8]{2,1,0:T(1,128)S(1)}, u32[]{:S(2)}, u32[]{:S(2)}) async-start(s32[32,1,8]{2,1,0:T(1,128)} %broadcast_in_dim.43), calls=%async_computation | async-start | bytes 32768 | tf_op jit(solution)/shard_map/all_to_all | solution.py:14
  26.4 9.2 all-to-all-start.1
  38.4 8.4 all-to-all-start.2
  46.9 13.8 %all-to-all-start.3 = ((bf16[4,16,4096]{2,1,0:T(8,128)(2,1)}), bf16[4,16,4096]{2,1,0:T(8,128)(2,1)S(1)}, u32[]{:S(2)}, u32[]{:S(2)}) async-start(bf16[4,16,4096]{2,1,0:T(8,128)(2,1)} %bitcast.11), calls=%async_computation.3 | async-start | bytes 1048576 | tf_op jit(solution)/shard_map/all_to_all | solution.py:133
  50.3 91.9 %reduce-scatter.4.cloned.1.call-start = ((), (), s32[]{:S(2)}) async-start(), calls=%async_computation.10 | async-start | bytes 10485760 | tf_op jit(solution)/shard_map/reduce_scatter | solution.py:52
  66.2 169.9 %copy-start.3 = (f32[4,4096]{1,0:T(4,128)S(1)}, f32[4,4096]{1,0:T(4,128)}, u32[]{:S(2)}) copy-start(f32[4,4096]{1,0:T(4,128)} %param.16) | copy-start | bytes 196612
  66.2 254.7 %copy-start.2 = (bf16[8,4096]{1,0:T(8,128)(2,1)S(1)}, bf16[8,4096]{1,0:T(8,128)(2,1)}, u32[]{:S(2)}) copy-start(bf16[8,4096]{1,0:T(8,128)(2,1)} %param.15) | copy-start | bytes 196612
  66.2 107.8 %reduce-scatter.6.cloned.1.call-start = ((), (), s32[]{:S(2)}) async-start(), calls=%async_computation.11 | async-start | bytes 2621440 | tf_op jit(solution)/shard_map/reduce_scatter | solution.py:52
  142.3 51.0 %reduce-scatter.8.cloned.1.call-start = ((), (), s32[]{:S(2)}) async-start(), calls=%async_computation.12 | async-start | bytes 786432 | tf_op jit(solution)/shard_map/reduce_scatter | solution.py:52
  174.0 62.0 %all-gather.5.cloned.1.call-start = ((), (), s32[]{:S(2)}) async-start(), calls=%async_computation.13 | async-start | bytes 2621440 | tf_op jit(solution)/shard_map/all_gather | solution.py:59
  203.5 117.4 %all-gather.7.cloned.1.call-start = ((), (), s32[]{:S(2)}) async-start(), calls=%async_computation.14 | async-start | bytes 10485760 | tf_op jit(solution)/shard_map/all_gather | solution.py:59
  362.7 130.7 %all-to-all-start.4 = ((bf16[32,1024,128]{2,1,0:T(8,128)(2,1)}), bf16[32,1024,128]{2,1,0:T(8,128)(2,1)}, u32[]{:S(2)}, u32[]{:S(2)}) async-start(bf16[32,1024,128]{2,1,0:T(8,128)(2,1)} %stack.6), calls=%async_computation.7 | async-start | bytes 16777216 | tf_op jit(solution)/shard_map/all_to_all | solution.py:162
  559.7 128.2 %all-to-all-start.5 = ((bf16[32,1024,128]{2,1,0:T(8,128)(2,1)}), bf16[32,1024,128]{2,1,0:T(8,128)(2,1)}, u32[]{:S(2)}, u32[]{:S(2)}) async-start(bf16[32,1024,128]{2,1,0:T(8,128)(2,1)} %stack.7), calls=%async_computation.8 | async-start | bytes 16777216 | tf_op jit(solution)/shard_map/all_to_all | solution.py:162
  911.8 14.7 %copy-start.1 = (bf16[32,4096]{1,0:T(8,128)(2,1)S(1)}, bf16[32,4096]{1,0:T(8,128)(2,1)}, u32[]{:S(2)}) copy-start(bf16[32,4096]{1,0:T(8,128)(2,1)} %param.13) | copy-start | bytes 786436
Sparse Core Ops, SparseCore 0:
  66.3 75.9 reduce-scatter.3
  144.7 29.2 reduce-scatter.5
  176.4 16.8 reduce-scatter.7
  203.6 32.3 all-gather.4
  237.6 83.2 all-gather.6
